TPU v7x, 32 devices: a whole 2x2x4 slice. The times are simulated.
32 devices in a mesh: grp: 2 (over y), gy: 4 (over z), gx: 2 (over x), gz: 2 (over core).
Axes of the slice: x: 2, y: 2, z: 4, core: 2. Of those that a mesh axis runs over, the one named last changes fastest.
Arguments:
- pair: bfloat16 [1024, 512, 128], P(('grp', 'gx', 'gz'), 'gy'), parts along dimension 0, may hold values from -6 to 6
- lengths: int32 [2], P('grp'), parts along dimension 0, may hold values from 256 to 512
- ln_gain: float32 [128], replicated, may hold values from 0.1 to 1.9
- ln_bias: float32 [128], replicated, may hold values from -3 to 3
- w_ab: bfloat16 [128, 512], replicated, may hold values from -0.5 to 0.5
- w_gate: bfloat16 [128, 128], replicated, may hold values from -0.5 to 0.5
- out_gain: float32 [128], replicated, may hold values from 0.1 to 1.9
- out_bias: float32 [128], replicated, may hold values from -3 to 3
- w_out: bfloat16 [128, 128], replicated, may hold values from -0.5 to 0.5
Outputs:
- update: bfloat16 [1024, 512, 128], P(('grp', 'gx', 'gz'), 'gy'), parts along dimension 0
There are 2 independent parts, one for each index of `grp`. A program takes and returns all parts, laid end to end along the dimension named above; an argument that names none is the same for every part. Nothing has to cross between parts.
Inputs may be any that keep to these rules, and one draw needn't show every extreme that they name: Residues from lengths[0] on are padding.
All inputs are finite; a program needn't handle non-finite values.
Results may differ from a plain program's by a relative error of at most 0.0052.
Values may be sent and summed in bfloat16 or wider, within the bound.
A program may use at most 128 MiB of HBM per device.

v0:
```python
import jax
import jax.numpy as jnp
from jax import lax
from jax.sharding import PartitionSpec as P


def layer_norm(values, gain, bias):
    values = values.astype(jnp.float32)
    mean = jnp.mean(values, -1, keepdims=True)
    spread = jnp.mean(jnp.square(values - mean), -1, keepdims=True)
    return (values - mean) * lax.rsqrt(spread + 1e-05) * gain + bias


def channel_norm(values, gain, bias):
    mean = jnp.mean(values, 0, keepdims=True)
    spread = jnp.mean(jnp.square(values - mean), 0, keepdims=True)
    return (values - mean) * lax.rsqrt(spread + 1e-05) * gain[:, None, None] + bias[:, None, None]


def body(pair, lengths, ln_gain, ln_bias, w_ab, w_gate, out_gain, out_bias, w_out):
    tile_rows, tile_cols, width = pair.shape
    hidden = w_out.shape[0]
    row_start = lax.axis_index(("gx", "gz")) * tile_rows
    col_index = lax.axis_index("gy")
    col_start = col_index * tile_cols
    normed = layer_norm(pair, ln_gain, ln_bias).astype(jnp.bfloat16)
    flat = normed.reshape(tile_rows * tile_cols, width)
    proj = jnp.dot(flat, w_ab, preferred_element_type=jnp.float32).reshape(
        tile_rows, tile_cols, 4 * hidden
    )
    row_live = (row_start + jnp.arange(tile_rows, dtype=jnp.int32) < lengths[0]).astype(jnp.float32)
    col_live = (col_start + jnp.arange(tile_cols, dtype=jnp.int32) < lengths[0]).astype(jnp.float32)
    pair_mask = (row_live[:, None] * col_live[None, :])[..., None]
    left = (pair_mask * jax.nn.sigmoid(proj[..., :hidden]) * proj[..., hidden : 2 * hidden]).astype(
        jnp.bfloat16
    )
    right = (
        pair_mask * jax.nn.sigmoid(proj[..., 2 * hidden : 3 * hidden]) * proj[..., 3 * hidden :]
    ).astype(jnp.bfloat16)
    left_major = jnp.transpose(left, (2, 0, 1))
    right_major = jnp.transpose(right, (2, 0, 1))
    column_rows = lax.all_gather(right_major, ("gx", "gz"), axis=1, tiled=True)
    right_mine = lax.all_to_all(column_rows, "gy", split_axis=1, concat_axis=2, tiled=True)
    triangle = jnp.einsum(
        "cik,cjk->cij",
        lax.all_gather(left_major, "gy", axis=2, tiled=True),
        right_mine,
        preferred_element_type=jnp.float32,
    )
    tri_norm = channel_norm(triangle, out_gain, out_bias).astype(jnp.bfloat16)
    gate = jax.nn.sigmoid(jnp.dot(flat, w_gate, preferred_element_type=jnp.float32)).reshape(
        tile_rows, tile_cols, width
    )
    projected = jnp.einsum("cij,cd->ijd", tri_norm, w_out, preferred_element_type=jnp.float32)
    return (gate * projected).astype(jnp.bfloat16)


def solution(mesh):
    in_specs = (P(("grp", "gx", "gz"), "gy", None), P("grp"), P(), P(), P(), P(), P(), P(), P())
    out_specs = P(("grp", "gx", "gz"), "gy", None)
    return jax.shard_map(body, mesh=mesh, in_specs=in_specs, out_specs=out_specs, check_vma=False)
```

profile of v0, /device:TPU:0, one launch (start us, length us, event | category | flops | bytes accessed | tf_op | source)
XLA Modules:
  0.0 898.8 jit_solution(9406988459465322010)
XLA Ops:
  7.4 3.8 convert_reduce_fusion
  11.2 6.0 fusion.5
  17.2 0.1 broadcast_multiply_fusion
  17.4 4.9 fusion.8
  22.3 13.1 %fusion.25 = f32[128,128,512]{2,1,0:T(8,128)} fusion(bf16[128,128,128]{2,1,0:T(8,128)(2,1)S(1)} %fusion.8, bf16[128,512]{1,0:T(8,128)(2,1)S(1)} %copy-done), kind=kOutput, calls=%fused_computation.34 | convolution fusion | flops 2147483648 | bytes 37879808 | tf_op jit(solution)/shard_map/dot_general | solution.py:28
  35.5 15.6 %fusion.22 = (bf16[128,128,128]{0,2,1:T(8,128)(2,1)}, bf16[128,128,128]{0,2,1:T(8,128)(2,1)}) fusion(f32[128,128,512]{2,1,0:T(8,128)} %fusion.25, f32[128,128]{1,0:T(8,128)S(1)} %broadcast_multiply_fusion), kind=kLoop, calls=%fused_computation.33 | loop fusion | flops 25165824 | bytes 42008576 | tf_op jit(solution)/shard_map/transpose | solution.py:41
  51.1 6.4 copy.13
  57.4 0.0 all-gather.5.cloned.1.call-update
  57.5 0.0 all-gather.3.cloned.1.call-start
  57.5 0.7 all-gather.3.cloned.1.call-update
  58.2 108.0 %all-gather.5.cloned.1.call-done = bf16[128,512,128]{2,0,1:T(8,128)(2,1)} async-done(((bf16[128,128,128]{2,0,1:T(8,128)(2,1)}), bf16[128,512,128]{2,0,1:T(8,128)(2,1)}) %all-gather.5.cloned.1.call-update) | async-done | bytes 16777232 | tf_op jit(solution)/shard_map/all_gather | solution.py:42
  166.2 7.3 all-to-all-start
  173.5 9.0 %fusion.2 = f32[16384,128]{1,0:T(8,128)} fusion(bf16[16384,128]{1,0:T(8,128)(2,1)} %bitcast.24, bf16[128,128]{1,0:T(8,128)(2,1)S(1)} %copy-done.10), kind=kOutput, calls=%fused_computation.3 | convolution fusion | flops 543162368 | bytes 12615680 | tf_op jit(solution)/shard_map/dot_general | solution.py:51
  182.5 580.3 %all-gather.3.cloned.1.call-done = bf16[128,128,512]{0,2,1:T(8,128)(2,1)} async-done(((bf16[128,128,128]{0,2,1:T(8,128)(2,1)}), bf16[128,128,512]{0,2,1:T(8,128)(2,1)}) %all-gather.3.cloned.1.call-update) | async-done | bytes 16777232 | tf_op jit(solution)/shard_map/all_gather | solution.py:46
  762.8 23.4 %copy.15 = bf16[128,128,512]{2,1,0:T(8,128)(2,1)} copy(bf16[128,128,512]{0,2,1:T(8,128)(2,1)} %all-gather.3.cloned.1.call-done) | data formatting | bytes 33554432 | tf_op jit(solution)/shard_map/all_gather | solution.py:46
  786.2 20.3 %all-to-all-done = bf16[128,512,128]{2,0,1:T(8,128)(2,1)} async-done(((bf16[128,512,128]{2,0,1:T(8,128)(2,1)}), bf16[128,512,128]{2,0,1:T(8,128)(2,1)}, u32[]{:S(2)}, u32[]{:S(2)}) %all-to-all-start) | async-done | bytes 16777248 | tf_op jit(solution)/shard_map/all_to_all | solution.py:43
  806.5 22.0 %copy.22 = bf16[128,4,128,128]{3,1,2,0:T(4,128)(2,1)} copy(bf16[128,4,128,128]{3,0,2,1:T(8,128)(2,1)} %bitcast.6) | data formatting | bytes 33554432 | tf_op jit(solution)/shard_map/all_to_all | solution.py:43
  828.6 24.9 %all_to_all.16 = bf16[128,128,512]{2,1,0:T(8,128)(2,1)} reshape(bf16[128,128,4,128]{3,2,1,0:T(4,128)(2,1)} %bitcast.23) | data formatting | bytes 33554432 | tf_op jit(solution)/shard_map/all_to_all | solution.py:43
  853.4 16.4 %fusion.28 = (f32[128,128]{1,0:T(8,128)S(1)}, f32[128,128,128]{2,1,0:T(8,128)}) fusion(bf16[128,128,512]{2,1,0:T(8,128)(2,1)} %copy.15, bf16[128,128,512]{2,1,0:T(8,128)(2,1)} %all_to_all.16), kind=kOutput, calls=%fused_computation.44 | convolution fusion | flops 2149564416 | bytes 42008576 | tf_op jit(solution)/shard_map/cik,cjk->cij/dot_general | solution.py:44
  869.8 4.4 multiply_reduce_fusion
  874.3 1.3 copy-done.2
  875.6 2.0 add_convert_fusion
  877.6 0.0 copy-start.1
  877.6 14.4 %multiply_convert_fusion = bf16[128,128,128]{2,1,0:T(8,128)(2,1)} fusion(f32[128,128,128]{2,1,0:T(8,128)} %bitcast.25, bf16[128,128,128]{2,1,0:T(8,128)(2,1)S(1)} %add_convert_fusion, bf16[128,128]{1,0:T(8,128)(2,1)S(1)} %copy-done.5), kind=kOutput, calls=%fused_computation.27 | convolution fusion | flops 541065216 | bytes 16809984 | tf_op jit(solution)/shard_map/cij,cd->ijd/dot_general | solution.py:54
  (26 shorter events, 0.1 us)
Async XLA Ops:
  6.5 15.8 %copy-start = (bf16[128,512]{1,0:T(8,128)(2,1)S(1)}, bf16[128,512]{1,0:T(8,128)(2,1)}, u32[]{:S(2)}) copy-start(bf16[128,512]{1,0:T(8,128)(2,1)} %param.13) | copy-start | bytes 393220
  6.5 10.8 %copy-start.7 = (f32[128]{0:T(128)S(1)}, f32[128]{0:T(128)}, u32[]{:S(2)}) copy-start(f32[128]{0:T(128)} %param.11) | copy-start | bytes 1540
  6.5 10.8 %copy-start.6 = (f32[128]{0:T(128)S(1)}, f32[128]{0:T(128)}, u32[]{:S(2)}) copy-start(f32[128]{0:T(128)} %param.12) | copy-start | bytes 1540
  6.5 159.7 %all-gather.5.cloned.1.call-start = ((), (), s32[]{:S(2)}) async-start(), calls=%async_computation.2 | async-start | bytes 20971520 | tf_op jit(solution)/shard_map/all_gather | solution.py:42
  6.6 10.8 %copy-start.3 = (bf16[128,128,128]{2,1,0:T(8,128)(2,1)S(1)}, bf16[128,128,128]{2,1,0:T(8,128)(2,1)}, u32[]{:S(2)}) copy-start(bf16[128,128,128]{2,1,0:T(8,128)(2,1)} %param.9) | copy-start | bytes 12582916
  22.3 13.2 %copy-start.4 = (bf16[128,128,128]{2,1,0:T(8,128)(2,1)}, bf16[128,128,128]{2,1,0:T(8,128)(2,1)S(1)}, u32[]{:S(2)}) copy-start(bf16[128,128,128]{2,1,0:T(8,128)(2,1)S(1)} %fusion.8) | copy-start | bytes 12582916
  57.5 705.3 %all-gather.3.cloned.1.call-start = ((), (), s32[]{:S(2)}) async-start(), calls=%async_computation.1 | async-start | bytes 20971520 | tf_op jit(solution)/shard_map/all_gather | solution.py:46
  58.2 115.3 %copy-start.10 = (bf16[128,128]{1,0:T(8,128)(2,1)S(1)}, bf16[128,128]{1,0:T(8,128)(2,1)}, u32[]{:S(2)}) copy-start(bf16[128,128]{1,0:T(8,128)(2,1)} %param.14) | copy-start | bytes 98308
  166.2 640.3 %all-to-all-start = ((bf16[128,512,128]{2,0,1:T(8,128)(2,1)}), bf16[128,512,128]{2,0,1:T(8,128)(2,1)}, u32[]{:S(2)}, u32[]{:S(2)}) async-start(bf16[128,512,128]{2,0,1:T(8,128)(2,1)} %all-gather.5.cloned.1.call-done), calls=%async_computation | async-start | bytes 33554432 | tf_op jit(solution)/shard_map/all_to_all | solution.py:43
  869.8 5.8 copy-start.2
  869.8 5.8 copy-start.8
  869.8 5.8 copy-start.9
  874.2 3.3 copy-start.5
  877.6 14.4 %copy-start.1 = (bf16[128,512]{1,0:T(8,128)(2,1)S(1)}, bf16[128,512]{1,0:T(8,128)(2,1)}, u32[]{:S(2)}) copy-start(bf16[128,512]{1,0:T(8,128)(2,1)} %param.13) | copy-start | bytes 393220
Sparse Core Ops, SparseCore 0:
  57.6 108.6 all-gather.4
  167.8 594.9 all-gather.2
where the time goes:
time: 900 us; the launch traced here: 899 us
  waiting for transfers between devices  709 us (79%)
  local copies, waits for them, and re-layouts  78 us (9%)
  matrix products  52.9 us (6%)
  other arithmetic  36.9 us (4%)
  between operations  14.4 us (2%)
    all_gather x1, waiting for transfers between devices, body(): lax.all_gather(left_major, 'gy', axis=2, tiled=True)  580 us
    all_gather x1, waiting for transfers between devices, body(): column_rows = lax.all_gather(right_major, ('gx', 'gz'), axis=1, tiled=True)  108 us
    all_to_all x2, local copies, waits for them, and re-layouts, body(): lax.all_to_all(column_rows, 'gy', split_axis=1, concat_axis=2, tiled=True)  46.9 us
    all_gather x1, local copies, waits for them, and re-layouts, body(): lax.all_gather(left_major, 'gy', axis=2, tiled=True)  23.4 us
    all_to_all x1, waiting for transfers between devices, body(): lax.all_to_all(column_rows, 'gy', split_axis=1, concat_axis=2, tiled=True)  20.3 us
  transfers between devices with their start and end apart: 3, of which 3 were waited for; matrix products, arithmetic and copies ran while one was open for 4% of the time, Pallas kernels for 0%

commit v1 on v0

--- a/solution.py
+++ b/solution.py
@@ -41,12 +41,37 @@
     right_major = jnp.transpose(right, (2, 0, 1))
     column_rows = lax.all_gather(right_major, ("gx", "gz"), axis=1, tiled=True)
     right_mine = lax.all_to_all(column_rows, "gy", split_axis=1, concat_axis=2, tiled=True)
+    formed, lower, val2 = (lax.axis_size("gy"), lax.axis_index("gy"), left_major.shape[2])
+    chunks = [(t, (t + 1) % formed) for t in range(formed)]
+    sheets = [(t, (t - 1) % formed) for t in range(formed)]
+    even = formed // 2
+    x_next = main = left_major
     triangle = jnp.einsum(
         "cik,cjk->cij",
-        lax.all_gather(left_major, "gy", axis=2, tiled=True),
-        right_mine,
+        left_major,
+        lax.dynamic_slice_in_dim(right_mine, lower * val2, left_major.shape[2], axis=2),
         preferred_element_type=jnp.float32,
     )
+    for w in range(1, even + 1):
+        x_next = lax.ppermute(x_next, axis_name="gy", perm=chunks)
+        if w < formed - even:
+            main = lax.ppermute(main, axis_name="gy", perm=sheets)
+            triangle = triangle + jnp.einsum(
+                "cik,cjk->cij",
+                main,
+                lax.dynamic_slice_in_dim(
+                    right_mine, (lower + w) % formed * val2, main.shape[2], axis=2
+                ),
+                preferred_element_type=jnp.float32,
+            )
+        triangle = triangle + jnp.einsum(
+            "cik,cjk->cij",
+            x_next,
+            lax.dynamic_slice_in_dim(
+                right_mine, (lower - w) % formed * val2, x_next.shape[2], axis=2
+            ),
+            preferred_element_type=jnp.float32,
+        )
     tri_norm = channel_norm(triangle, out_gain, out_bias).astype(jnp.bfloat16)
     gate = jax.nn.sigmoid(jnp.dot(flat, w_gate, preferred_element_type=jnp.float32)).reshape(
         tile_rows, tile_cols, width

time: 900 us -> 937 us (1.041)
  starting transfers between devices: 7.32 us -> 188 us
  waiting for transfers between devices: 709 us -> 532 us
  matrix products: 52.9 us -> 77.2 us
    all_gather x1 -> x0, waiting for transfers between devices: 580 us -> none  [body(): lax.all_gather(left_major, 'gy', axis=2, tiled=True)]
    ppermute x0 -> x3, waiting for transfers between devices: none -> 423 us  [the longest x2 423 us: body(): x_next = lax.ppermute(x_next, axis_name='gy', perm=chunks)]
    ppermute x0 -> x3, starting transfers between devices: none -> 181 us  [the longest x2 179 us: body(): x_next = lax.ppermute(x_next, axis_name='gy', perm=chunks)]
    dot_general x1 -> x4, matrix products: 16.4 us -> 41.9 us  [the longest x2 25.5 us: body(): jnp.einsum('cik,cjk->cij', x_next, lax.dynamic_slice_in_dim(right_mine, (...]
    all_gather x1 -> x0, local copies, waits for them, and re-layouts: 23.4 us -> none  [body(): lax.all_gather(left_major, 'gy', axis=2, tiled=True)]
    all_to_all x1, waiting for transfers between devices: 20.3 us -> 0.01 us  [body(): lax.all_to_all(column_rows, 'gy', split_axis=1, concat_axis=2, tiled=True)]
    ppermute x0 -> x3, local copies, waits for them, and re-layouts: none -> 20.2 us  [the longest x2 13.4 us: body(): x_next = lax.ppermute(x_next, axis_name='gy', perm=chunks)]
  transfers between devices with their start and end apart: 3 -> 5, of which waited for: 3 -> 3; matrix products, arithmetic and copies ran while one was open for 4% -> 4% of each run, Pallas kernels for 0% -> 0%
where the time goes in v1:
time: 937 us; the launch traced here: 929 us
  waiting for transfers between devices  532 us (57%)
  starting transfers between devices  188 us (20%)
  local copies, waits for them, and re-layouts  81.6 us (9%)
  matrix products  77.2 us (8%)
  other arithmetic  36.7 us (4%)
  between operations  14.4 us (2%)
    ppermute x2, waiting for transfers between devices, body(): x_next = lax.ppermute(x_next, axis_name='gy', perm=chunks)  423 us
    ppermute x2, starting transfers between devices, body(): x_next = lax.ppermute(x_next, axis_name='gy', perm=chunks)  179 us
    all_gather x1, waiting for transfers between devices, body(): column_rows = lax.all_gather(right_major, ('gx', 'gz'), axis=1, tiled=True)  109 us
    all_to_all x2, local copies, waits for them, and re-layouts, body(): lax.all_to_all(column_rows, 'gy', split_axis=1, concat_axis=2, tiled=True)  46.9 us
    dot_general x2, matrix products, body(): jnp.einsum('cik,cjk->cij', x_next, lax.dynamic_slice_in_dim(right_mine, (...  25.5 us
  transfers between devices with their start and end apart: 5, of which 3 were waited for; matrix products, arithmetic and copies ran while one was open for 4% of the time, Pallas kernels for 0%

profile of v1, /device:TPU:0, one launch (start us, length us, event | category | flops | bytes accessed | tf_op | source)
XLA Modules:
  0.0 929.4 jit_solution(4321652877712087150)
XLA Ops:
  7.4 3.8 convert_reduce_fusion
  11.2 6.0 fusion.5
  17.4 4.9 fusion.8
  22.3 13.1 %fusion.35 = f32[128,128,512]{2,1,0:T(8,128)} fusion(bf16[128,128,128]{2,1,0:T(8,128)(2,1)S(1)} %fusion.8, bf16[128,512]{1,0:T(8,128)(2,1)S(1)} %copy-done), kind=kOutput, calls=%fused_computation.43 | convolution fusion | flops 2147483648 | bytes 37879808 | tf_op jit(solution)/shard_map/dot_general | solution.py:28
  35.5 15.4 %fusion.30 = (bf16[128,128,128]{0,2,1:T(8,128)(2,1)}, bf16[128,128,128]{0,2,1:T(8,128)(2,1)}) fusion(f32[128,128,512]{2,1,0:T(8,128)} %fusion.35, f32[128,128]{1,0:T(8,128)S(1)} %broadcast_multiply_fusion), kind=kLoop, calls=%fused_computation.42 | loop fusion | flops 25165824 | bytes 42008576 | tf_op jit(solution)/shard_map/transpose | solution.py:41
  50.9 6.4 copy.16
  57.3 108.8 %all-gather.2.cloned.1.call-done = bf16[128,512,128]{2,0,1:T(8,128)(2,1)} async-done(((bf16[128,128,128]{2,0,1:T(8,128)(2,1)}), bf16[128,512,128]{2,0,1:T(8,128)(2,1)}) %all-gather.2.cloned.1.call-update) | async-done | bytes 16777232 | tf_op jit(solution)/shard_map/all_gather | solution.py:42
  166.1 7.0 all-to-all-start
  177.0 361.4 %collective-permute-done.1 = bf16[128,128,128]{0,2,1:T(8,128)(2,1)} collective-permute-done((bf16[128,128,128]{0,2,1:T(8,128)(2,1)}, bf16[128,128,128]{0,2,1:T(8,128)(2,1)}, u32[]{:S(2)}, u32[]{:S(2)}) %collective-permute-start.1) | collective-permute-done | bytes 4194336 | tf_op jit(solution)/shard_map/ppermute | solution.py:56
  538.3 176.7 %collective-permute-start.2 = (bf16[128,128,128]{0,2,1:T(8,128)(2,1)}, bf16[128,128,128]{0,2,1:T(8,128)(2,1)}, u32[]{:S(2)}, u32[]{:S(2)}) collective-permute-start(bf16[128,128,128]{0,2,1:T(8,128)(2,1)} %collective-permute-done.1), channel_id=1, source_target_pairs={{0,4},{4,8},{8,12},{12,0},{1,5},{5,9},{9,13},{13,1},{2,6},{6,10},{... | collective-permute-start | bytes 12582920 | tf_op jit(solution)/shard_map/ppermute | solution.py:56
  715.0 6.7 copy.18
  721.8 7.8 fusion.2
  729.5 6.7 copy.20
  736.2 6.8 copy.19
  743.0 61.7 %collective-permute-done.2 = bf16[128,128,128]{0,2,1:T(8,128)(2,1)} collective-permute-done((bf16[128,128,128]{0,2,1:T(8,128)(2,1)}, bf16[128,128,128]{0,2,1:T(8,128)(2,1)}, u32[]{:S(2)}, u32[]{:S(2)}) %collective-permute-start.2) | collective-permute-done | bytes 4194336 | tf_op jit(solution)/shard_map/ppermute | solution.py:56
  804.7 6.7 copy.21
  811.5 22.0 %copy.28 = bf16[128,4,128,128]{3,1,2,0:T(4,128)(2,1)} copy(bf16[128,4,128,128]{3,0,2,1:T(8,128)(2,1)} %bitcast.6) | data formatting | bytes 33554432 | tf_op jit(solution)/shard_map/all_to_all | solution.py:43
  833.5 24.9 %all_to_all.16 = bf16[128,128,512]{2,1,0:T(8,128)(2,1)} reshape(bf16[128,128,4,128]{3,2,1,0:T(4,128)(2,1)} %bitcast.25) | data formatting | bytes 33554432 | tf_op jit(solution)/shard_map/all_to_all | solution.py:43
  858.4 10.1 %fusion.25 = f32[128,128,128]{2,1,0:T(8,128)} fusion(bf16[128,128,128]{2,1,0:T(8,128)(2,1)} %copy.19, bf16[128,128,512]{2,1,0:T(8,128)(2,1)} %all_to_all.16, s32[]{:T(128)S(6)} %select_n.29), kind=kOutput, calls=%fused_computation.37 | convolution fusion | flops 536870912 | bytes 16777220 | tf_op jit(solution)/shard_map/cik,cjk->cij/dot_general | solution.py:59
  868.6 8.6 fusion.23
  877.2 6.2 fusion.27
  883.5 16.9 %fusion.42 = (f32[128,128]{1,0:T(8,128)S(1)}, f32[128,128,128]{2,1,0:T(8,128)}) fusion(bf16[128,128,128]{2,1,0:T(8,128)(2,1)} %copy.21, bf16[128,128,512]{2,1,0:T(8,128)(2,1)} %all_to_all.16, s32[]{:T(128)S(6)} %select_n.33, f32[128,128,128]{2,1,0:T(8,128)} %fusion.23, f32[128,128,128]{2,1,0:T(8,128)} %fusion.27, f32[128,128,128]{2,1,0:T(8,128)} %fusion.25), kind=kOutput, calls=%fused_computation.57 | convolution fusion | flops 545243136 | bytes 42008580 | tf_op jit(solution)/shard_map/cik,cjk->cij/dot_general | solution.py:67
  900.3 4.4 multiply_reduce_fusion
  908.1 14.4 %multiply_convert_fusion = bf16[128,128,128]{2,1,0:T(8,128)(2,1)} fusion(f32[128,128,128]{2,1,0:T(8,128)} %bitcast.27, bf16[128,128,128]{2,1,0:T(8,128)(2,1)S(1)} %add_convert_fusion, bf16[128,128]{1,0:T(8,128)(2,1)S(1)} %copy-done.7), kind=kOutput, calls=%fused_computation.27 | convolution fusion | flops 541065216 | bytes 16809984 | tf_op jit(solution)/shard_map/cij,cd->ijd/dot_general | solution.py:79
  (39 shorter events, 7.4 us)
Async XLA Ops:
  6.5 15.8 %copy-start = (bf16[128,512]{1,0:T(8,128)(2,1)S(1)}, bf16[128,512]{1,0:T(8,128)(2,1)}, u32[]{:S(2)}) copy-start(bf16[128,512]{1,0:T(8,128)(2,1)} %param.13) | copy-start | bytes 393220
  6.5 10.8 %copy-start.9 = (f32[128]{0:T(128)S(1)}, f32[128]{0:T(128)}, u32[]{:S(2)}) copy-start(f32[128]{0:T(128)} %param.11) | copy-start | bytes 1540
  6.5 10.8 %copy-start.8 = (f32[128]{0:T(128)S(1)}, f32[128]{0:T(128)}, u32[]{:S(2)}) copy-start(f32[128]{0:T(128)} %param.12) | copy-start | bytes 1540
  6.5 159.6 %all-gather.2.cloned.1.call-start = ((), (), s32[]{:S(2)}) async-start(), calls=%async_computation.1 | async-start | bytes 20971520 | tf_op jit(solution)/shard_map/all_gather | solution.py:42
  6.6 10.8 %copy-start.4 = (bf16[128,128,128]{2,1,0:T(8,128)(2,1)S(1)}, bf16[128,128,128]{2,1,0:T(8,128)(2,1)}, u32[]{:S(2)}) copy-start(bf16[128,128,128]{2,1,0:T(8,128)(2,1)} %param.9) | copy-start | bytes 12582916
  22.3 13.2 %copy-start.5 = (bf16[128,128,128]{2,1,0:T(8,128)(2,1)}, bf16[128,128,128]{2,1,0:T(8,128)(2,1)S(1)}, u32[]{:S(2)}) copy-start(bf16[128,128,128]{2,1,0:T(8,128)(2,1)S(1)} %fusion.8) | copy-start | bytes 12582916
  166.1 645.4 %all-to-all-start = ((bf16[128,512,128]{2,0,1:T(8,128)(2,1)}), bf16[128,512,128]{2,0,1:T(8,128)(2,1)}, u32[]{:S(2)}, u32[]{:S(2)}) async-start(bf16[128,512,128]{2,0,1:T(8,128)(2,1)} %all-gather.2.cloned.1.call-done), calls=%async_computation | async-start | bytes 33554432 | tf_op jit(solution)/shard_map/all_to_all | solution.py:43
  173.1 548.7 %copy-start.12 = (bf16[128,128]{1,0:T(8,128)(2,1)S(1)}, bf16[128,128]{1,0:T(8,128)(2,1)}, u32[]{:S(2)}) copy-start(bf16[128,128]{1,0:T(8,128)(2,1)} %param.14) | copy-start | bytes 98308
  173.1 365.2 %collective-permute-start.1 = (bf16[128,128,128]{0,2,1:T(8,128)(2,1)}, bf16[128,128,128]{0,2,1:T(8,128)(2,1)}, u32[]{:S(2)}, u32[]{:S(2)}) collective-permute-start(bf16[128,128,128]{0,2,1:T(8,128)(2,1)} %get-tuple-element.6), channel_id=1, source_target_pairs={{0,4},{4,8},{8,12},{12,0},{1,5},{5,9},{9,13},{13,1},{2,6},{6,10},{... | collective-permute-start | bytes 12582920 | tf_op jit(solution)/shard_map/ppermute | solution.py:56
  175.1 561.2 %collective-permute-start = (bf16[128,128,128]{0,2,1:T(8,128)(2,1)}, bf16[128,128,128]{0,2,1:T(8,128)(2,1)}, u32[]{:S(2)}, u32[]{:S(2)}) collective-permute-start(bf16[128,128,128]{0,2,1:T(8,128)(2,1)} %get-tuple-element.6), channel_id=1, source_target_pairs={{0,12},{4,0},{8,4},{12,8},{1,13},{5,1},{9,5},{13,9},{2,14},{6,2},{... | collective-permute-start | bytes 12582920 | tf_op jit(solution)/shard_map/ppermute | solution.py:58
  538.3 266.4 %collective-permute-start.2 = (bf16[128,128,128]{0,2,1:T(8,128)(2,1)}, bf16[128,128,128]{0,2,1:T(8,128)(2,1)}, u32[]{:S(2)}, u32[]{:S(2)}) collective-permute-start(bf16[128,128,128]{0,2,1:T(8,128)(2,1)} %collective-permute-done.1), channel_id=1, source_target_pairs={{0,4},{4,8},{8,12},{12,0},{1,5},{5,9},{9,13},{13,1},{2,6},{6,10},{... | collective-permute-start | bytes 12582920 | tf_op jit(solution)/shard_map/ppermute | solution.py:56
  858.4 10.1 %copy-start.3 = (bf16[128,128,512]{2,1,0:T(8,128)(2,1)S(1)}, bf16[128,128,512]{2,1,0:T(8,128)(2,1)}, u32[]{:S(2)}) copy-start(bf16[128,128,512]{2,1,0:T(8,128)(2,1)} %all_to_all.16) | copy-start | bytes 50331652
  868.6 8.7 copy-start.6
  900.3 5.8 copy-start.2
  900.3 5.8 copy-start.10
  900.3 5.8 copy-start.11
  904.8 3.4 copy-start.7
  908.1 14.4 %copy-start.1 = (bf16[128,512]{1,0:T(8,128)(2,1)S(1)}, bf16[128,512]{1,0:T(8,128)(2,1)}, u32[]{:S(2)}) copy-start(bf16[128,512]{1,0:T(8,128)(2,1)} %param.13) | copy-start | bytes 393220
Sparse Core Ops, SparseCore 0:
  57.4 108.6 all-gather.1
